TPU v7x, 32 devices: a whole 2x2x4 slice. The times are simulated.
32 devices in a mesh: tok: 16 (over z, x, core), blk: 2 (over y).
Axes of the slice: x: 2, y: 2, z: 4, core: 2. Of those that a mesh axis runs over, the one named last changes fastest.
Arguments:
- activations: bfloat16 [2048, 7168], P('tok', 'blk'), may hold values from -600 to 600
- signs: float32 [7168], P('blk'), may hold values from -1 to 1, as said below
Outputs:
- hessian: float32 [7168, 7168], P('tok', 'blk')
- incoherence: float32 [7168], P('blk')
- largest_ratio: float32 [], replicated
Inputs may be any that keep to these rules, and one draw needn't show every extreme that they name: `signs`: every entry is -1 or 1.
All inputs are finite; a program needn't handle non-finite values.
Results may differ from a plain program's by a relative error of at most 0.0037.
Values may be sent and summed in bfloat16 or wider, within the bound.
A program may use at most 640 MiB of HBM per device.

v0:
```python
import functools
import math

import jax
import jax.numpy as jnp
import numpy as np
from jax import lax
from jax.experimental import pallas as pl
from jax.experimental.pallas import tpu as pltpu
from jax.sharding import PartitionSpec as P

WALSH = 512
MIX = 14
FEATURES = 7168

EPS = 1e-06
DAMP = 0.01

LANES = 128
UNIT_WALSH = LANES // math.gcd(LANES, MIX)
UNIT = UNIT_WALSH * MIX
MESH = pl.DeviceIdType.MESH


def parity(number):
    return bin(number).count("1") & 1


def unit_tables():
    walsh = np.array(
        [[1 - 2 * parity(i & j) for j in range(UNIT_WALSH)] for i in range(UNIT_WALSH)], np.float64
    )
    k = np.arange(MIX)[:, None]
    n = np.arange(MIX)[None, :]
    cosine = math.sqrt(2.0 / MIX) * np.cos(math.pi * (n + 0.5) * k / MIX)
    cosine[0] *= math.sqrt(0.5)
    table = np.kron(walsh, cosine.T).astype(np.float32)
    high = table.astype(jnp.bfloat16)
    low = (table - high.astype(np.float32)).astype(jnp.bfloat16)
    return high, low


def rotate_kernel(blocks, chunks, high_ref, low_ref, flips_ref, *refs):
    pieces, (out_ref, square_ref) = refs[:blocks], refs[blocks:]
    mixed = []
    for c in range(chunks):
        total = None
        for k in range(blocks):
            part = pieces[k][:, c * UNIT : (c + 1) * UNIT]
            value = jnp.dot(part, high_ref[...], preferred_element_type=jnp.float32)
            value += jnp.dot(part, low_ref[...], preferred_element_type=jnp.float32)
            value = value * flips_ref[0, k]
            total = value if total is None else total + value
        mixed.append(total)
    step = 1
    while step < chunks:
        for low in range(chunks):
            if not low & step:
                a, b = mixed[low], mixed[low | step]
                mixed[low], mixed[low | step] = a + b, a - b
        step *= 2
    square = jnp.float32(0.0)
    for c in range(chunks):
        rounded = (mixed[c] * (1.0 / math.sqrt(WALSH))).astype(jnp.bfloat16)
        out_ref[:, c * UNIT : (c + 1) * UNIT] = rounded
        wide = rounded.astype(jnp.float32)
        square += jnp.sum(wide * wide)
    square_ref[...] = jnp.full(square_ref.shape, square, jnp.float32)


def rotate(pieces, flips):
    blocks = len(pieces)
    rows, width = pieces[0].shape
    high, low = unit_tables()
    vmem = pl.BlockSpec(memory_space=pltpu.VMEM)
    return pl.pallas_call(
        functools.partial(rotate_kernel, blocks, width // UNIT),
        out_shape=(
            jax.ShapeDtypeStruct((rows, width), jnp.bfloat16),
            jax.ShapeDtypeStruct((8, LANES), jnp.float32),
        ),
        in_specs=[vmem, vmem, pl.BlockSpec(memory_space=pltpu.SMEM)] + [vmem] * blocks,
        out_specs=(vmem, vmem),
        compiler_params=pltpu.CompilerParams(vmem_limit_bytes=48 * 1024 * 1024),
        name="rotate",
    )(jnp.asarray(high), jnp.asarray(low), flips, *pieces)


def place(tok, row_count, width, window):
    first = tok * row_count
    owner = first // width
    offset = first - owner * width
    start = jnp.minimum(offset // LANES * LANES, width - window)
    return owner, start, offset - start


def greet_all(tok, blk):
    tokens, blocks = lax.axis_size("tok"), lax.axis_size("blk")
    count = tokens * blocks
    barrier = pltpu.get_barrier_semaphore()
    me = tok * blocks + blk

    @pl.loop(1, count)
    def _(k):
        other = lax.rem(me + k, count)
        pl.semaphore_signal(
            barrier, inc=1, device_id={"tok": other // blocks, "blk": other % blocks}, device_id_type=MESH
        )

    pl.semaphore_wait(barrier, count - 1)


def broadcast_start(tok, blk, src, dst, send, recv):
    tokens, blocks = lax.axis_size("tok"), lax.axis_size("blk")
    count = tokens * blocks
    me = tok * blocks + blk

    @pl.loop(1, count)
    def _(k):
        other = lax.rem(me + k, count)
        pltpu.make_async_remote_copy(
            src, dst.at[me], send, recv,
            device_id={"tok": other // blocks, "blk": other % blocks}, device_id_type=MESH,
        ).start()


def broadcast_wait(tok, blk, dst, send, recv):
    count = dst.shape[0] - 1
    both = pltpu.make_async_remote_copy(
        dst.at[pl.ds(0, count)], dst.at[pl.ds(0, count)], send, recv,
        device_id={"tok": tok, "blk": blk}, device_id_type=MESH,
    )
    both.wait_send()
    both.wait_recv()


def spread_kernel(src, dst, local, send, recv):
    tok, blk = lax.axis_index("tok"), lax.axis_index("blk")
    greet_all(tok, blk)
    broadcast_start(tok, blk, src, dst, send, recv)
    own = pltpu.make_async_copy(src, dst.at[tok * lax.axis_size("blk") + blk], local)
    own.start()
    own.wait()
    broadcast_wait(tok, blk, dst, send, recv)


def spread(block):
    count = lax.axis_size("tok") * lax.axis_size("blk")
    vmem = pl.BlockSpec(memory_space=pltpu.VMEM)
    return pl.pallas_call(
        spread_kernel,
        out_shape=jax.ShapeDtypeStruct((count,) + block.shape, block.dtype),
        in_specs=[vmem],
        out_specs=vmem,
        scratch_shapes=[pltpu.SemaphoreType.DMA] * 3,
        compiler_params=pltpu.CompilerParams(collective_id=1, has_side_effects=True),
        name="spread",
    )(block)


def gather_kernel(
    depth, across, sub, early, row_count, rot, part, cols, rows, parts,
    local, recv, pair_send, pair_recv, z_send, x_send, y_send, y_recv, part_local, part_send, part_recv,
):
    tok, blk = lax.axis_index("tok"), lax.axis_index("blk")
    blocks = lax.axis_size("blk")
    tok_rows, width = rot.shape
    window = rows.shape[1]
    half = cols.shape[0] // 2
    steps = tok_rows // sub
    core, chip = tok % 2, tok // 2
    z, x = chip // across, chip % across

    greet_all(tok, blk)
    own_rows = pltpu.make_async_copy(rot, cols.at[pl.ds(pl.multiple_of(tok * tok_rows, sub), tok_rows)], local)
    own_rows.start()

    def first_row(oz, ox, s):
        return pl.multiple_of(((oz * across + ox) * 2 + core) * tok_rows + s * sub, sub)

    def remote(src, dst, send, arrive, to_tok, to_blk):
        return pltpu.make_async_remote_copy(
            src, dst, send, arrive, device_id={"tok": to_tok, "blk": to_blk}, device_id_type=MESH
        )

    def fan(src, oz, ox, s, z_ways, x_ways):
        row = first_row(oz, ox, s)
        dst = cols.at[pl.ds(row, sub)]
        arrive = recv.at[(oz * across + ox) * steps + s]
        for way in x_ways:

            @pl.when((x + way >= 0) & (x + way < across))
            def _():
                remote(src, dst, x_send.at[(way + 1) // 2], arrive, tok + 2 * way, blk).start()

        for way in z_ways:

            @pl.when((z + way >= 0) & (z + way < depth))
            def _():
                remote(src, dst, z_send.at[(way + 1) // 2], arrive, tok + 2 * across * way, blk).start()

        remote(src, dst, pair_send, pair_recv, tok + 1 - 2 * core, blk).start()
        for j in range(2):
            owner, start, _ = place(chip * 2 + j, row_count, width, window)

            @pl.when(owner == blk)
            def _():
                part_src = src.at[:, pl.ds(pl.multiple_of(start, LANES), window)]
                for k in range(1, blocks):
                    remote(
                        part_src, rows.at[pl.ds(row, sub)], y_send.at[2 * k + j], y_recv,
                        chip * 2 + j, lax.rem(blk + k, blocks),
                    ).start()

    def relay(oz, ox, s, z_ways, x_ways):
        piece = cols.at[pl.ds(first_row(oz, ox, s), sub)]
        remote(piece, piece, pair_send, recv.at[(oz * across + ox) * steps + s], tok, blk).wait_recv()
        fan(piece, oz, ox, s, z_ways, x_ways)

    @pl.loop(0, steps)
    def _(s):
        fan(rot.at[pl.ds(pl.multiple_of(s * sub, sub), sub)], z, x, s, (1, -1), (1, -1))

    broadcast_start(tok, blk, part, parts, part_send, part_recv)
    own_part = pltpu.make_async_copy(part, parts.at[tok * blocks + blk], part_local)
    own_part.start()

    for dx in range(1, across):
        for way in (1, -1):
            ox = x - way * dx

            @pl.when((ox >= 0) & (ox < across))
            def _():
                for s in range(early):
                    relay(z, ox, s, (1, -1), (way,))

    for dz in range(1, depth):

        @pl.loop(early, steps)
        def _(s):
            for way in (1, -1):
                oz = z - way * dz

                @pl.when((oz >= 0) & (oz < depth))
                def _():
                    relay(oz, x, s, (way,), (1, -1))

        for way in (1, -1):
            oz = z - way * dz

            @pl.when((oz >= 0) & (oz < depth))
            def _():
                @pl.loop(0, across * early)
                def _(n):
                    relay(oz, n // early, n % early, (way,), ())

    for dx in range(1, across):
        for way in (1, -1):
            ox = x - way * dx

            @pl.when((ox >= 0) & (ox < across))
            def _():
                for dz in range(depth):
                    for side in (1, -1) if dz else (1,):
                        oz = z - side * dz

                        @pl.when((oz >= 0) & (oz < depth))
                        def _():
                            @pl.loop(early, steps)
                            def _(s):
                                relay(oz, ox, s, (), (way,))

    def settle(count, send):
        piece = cols.at[pl.ds(0, count)]
        remote(piece, piece, send, pair_recv, tok, blk).wait_send()

    late = steps - early
    for v in range(depth):
        @pl.when(z == v)
        def _():
            unit = (late + early * across) * sub
            if v < depth - 1:
                settle((v + 1) * unit, z_send.at[1])
            if v > 0:
                settle((depth - v) * unit, z_send.at[0])

    for v in range(across):
        @pl.when(x == v)
        def _():
            unit = (late * depth + early) * sub
            if v < across - 1:
                settle((v + 1) * unit, x_send.at[1])
            if v > 0:
                settle((across - v) * unit, x_send.at[0])

    settle(half, pair_send)
    for j in range(2):
        owner, _, _ = place(chip * 2 + j, row_count, width, window)

        @pl.when(owner == blk)
        def _():
            piece = rows.at[pl.ds(0, half)]
            for k in range(1, blocks):
                remote(piece, piece, y_send.at[2 * k + j], y_recv, tok, blk).wait_send()

    piece = cols.at[pl.ds(0, half)]
    remote(piece, piece, pair_send, pair_recv, tok, blk).wait_recv()
    owner, _, _ = place(tok, row_count, width, window)

    @pl.when(owner != blk)
    def _():
        remote(rows, rows, pair_send, y_recv, tok, blk).wait_recv()

    own_rows.wait()
    own_part.wait()
    broadcast_wait(tok, blk, parts, part_send, part_recv)


def gather(rotated, squares, window, row_count):
    tok_rows, width = rotated.shape
    groups, blocks = lax.axis_size("tok"), lax.axis_size("blk")
    depth = 4 if groups % 8 == 0 else 1
    across = groups // (2 * depth)
    sub = 16
    steps = tok_rows // sub
    dma = pltpu.SemaphoreType.DMA
    vmem = pl.BlockSpec(memory_space=pltpu.VMEM)
    anywhere = pl.BlockSpec(memory_space=pl.ANY)
    return pl.pallas_call(
        functools.partial(gather_kernel, depth, across, sub, 1, row_count),
        out_shape=(
            jax.ShapeDtypeStruct((groups * tok_rows, width), rotated.dtype),
            jax.ShapeDtypeStruct((groups * tok_rows, window), rotated.dtype),
            jax.ShapeDtypeStruct((groups * blocks,) + squares.shape, squares.dtype),
        ),
        in_specs=[vmem, vmem],
        out_specs=(anywhere, anywhere, vmem),
        scratch_shapes=[
            dma, dma((groups // 2 * steps,)), dma, dma, dma((2,)), dma((2,)), dma((2 * blocks,)), dma,
            dma, dma, dma,
        ],
        compiler_params=pltpu.CompilerParams(
            collective_id=0, has_side_effects=True, vmem_limit_bytes=16 * 1024 * 1024
        ),
        name="gather",
    )(rotated, squares)


def gram_kernel(rows, scale_ref, window_ref, all_ref, columns_ref, hessian_ref, peak_ref, best, left, sem):
    tile = pl.program_id(0)
    width = columns_ref.shape[1]
    tok, blk = lax.axis_index("tok"), lax.axis_index("blk")
    whole = window_ref.shape[1]
    block_width = all_ref.shape[1]
    owner, start, skew = place(tok, rows, block_width, whole)
    diagonal = tok * rows - blk * block_width - tile * width
    inverse = scale_ref[0, 0]

    @pl.when((tile == 0) & (owner == blk))
    def _():
        own = pltpu.make_async_copy(all_ref.at[:, pl.ds(pl.multiple_of(start, LANES), whole)], left, sem)
        own.start()
        own.wait()

    @pl.when((tile == 0) & (owner != blk))
    def _():
        given = pltpu.make_async_copy(window_ref, left, sem)
        given.start()
        given.wait()

    block = lax.dot_general(
        left[...], columns_ref[...], (((0,), (0,)), ((), ())), preferred_element_type=jnp.float32
    )
    if whole == rows:
        block = block[:rows]
    else:
        block = jnp.where(skew == 0, block[:rows], block[whole - rows :])
    row = lax.broadcasted_iota(jnp.int32, (rows, width), 0) + diagonal
    column = lax.broadcasted_iota(jnp.int32, (rows, width), 1)
    on_diag = row == column
    hessian_ref[...] = block * inverse + jnp.where(on_diag, DAMP, 0.0)
    size = jnp.where(on_diag, 0.0, jnp.abs(block))
    most = size[:, :LANES]
    for j in range(1, width // LANES):
        most = jnp.maximum(most, size[:, j * LANES : (j + 1) * LANES])

    @pl.when(tile == 0)
    def _():
        best[...] = most

    @pl.when(tile > 0)
    def _():
        best[...] = jnp.maximum(best[...], most)

    @pl.when(tile == pl.num_programs(0) - 1)
    def _():
        flat = jnp.max(best[...], axis=1, keepdims=True)
        turned = jnp.transpose(jnp.broadcast_to(flat, (rows, LANES)))
        peak_ref[...] = turned[:8] * inverse


def gram(window, columns, rows, inverse):
    tokens, width = columns.shape
    tile = 512 if width % 512 == 0 else LANES
    anywhere = pl.BlockSpec(memory_space=pl.ANY)
    return pl.pallas_call(
        functools.partial(gram_kernel, rows),
        grid=(width // tile,),
        out_shape=(
            jax.ShapeDtypeStruct((rows, width), jnp.float32),
            jax.ShapeDtypeStruct((8, rows), jnp.float32),
        ),
        in_specs=[
            pl.BlockSpec(memory_space=pltpu.SMEM),
            anywhere,
            anywhere,
            pl.BlockSpec((tokens, tile), lambda i: (0, i)),
        ],
        out_specs=(
            pl.BlockSpec((rows, tile), lambda i: (0, i)),
            pl.BlockSpec((8, rows), lambda i: (0, 0)),
        ),
        scratch_shapes=[
            pltpu.VMEM((rows, LANES), jnp.float32),
            pltpu.VMEM(window.shape, window.dtype),
            pltpu.SemaphoreType.DMA,
        ],
        compiler_params=pltpu.CompilerParams(vmem_limit_bytes=48 * 1024 * 1024),
        cost_estimate=pl.CostEstimate(
            flops=2 * rows * width * tokens,
            bytes_accessed=2 * tokens * width + 4 * rows * width,
            transcendentals=0,
        ),
        name="gram",
    )(inverse.reshape(1, 1), window, columns, columns)


def per_device(activations, signs):
    tok_rows, block_width = activations.shape
    blocks = lax.axis_size("blk")
    me = lax.axis_index("blk")
    token_groups = lax.axis_size("tok")
    signed = activations * signs.astype(jnp.bfloat16)[None, :]
    pieces, flips = [], []
    for k in range(blocks):
        piece = signed
        if k:
            piece = lax.ppermute(signed, "blk", [(i, i ^ k) for i in range(blocks)])
        pieces.append(piece)
        table = jnp.asarray([1.0 - 2.0 * parity(i & (i ^ k)) for i in range(blocks)], jnp.float32)
        flips.append(table[me])
    rotated, squares = rotate(pieces, jnp.stack(flips).reshape(1, blocks))
    row_count = FEATURES // token_groups
    window = -(-row_count // LANES) * LANES
    all_tokens, rows_window, parts = gather(rotated, squares, window, row_count)
    trace_total = jnp.sum(parts[:, 0, 0])
    diag_mean = trace_total / FEATURES + EPS
    hessian, peak = gram(rows_window, all_tokens, row_count, 1.0 / diag_mean)
    peaks = spread(peak)[:, 0, :]
    ratios = jnp.max(peaks.reshape(token_groups, blocks, row_count), axis=1).reshape(FEATURES)
    incoherence = lax.dynamic_slice_in_dim(ratios, me * block_width, block_width, 0)
    return (hessian, incoherence, jnp.max(ratios))


def solution(mesh):
    in_specs = (P("tok", "blk"), P("blk"))
    out_specs = (P("tok", "blk"), P("blk"), P())
    return jax.shard_map(
        per_device, mesh=mesh, in_specs=in_specs, out_specs=out_specs, check_vma=False
    )
```

profile of v0, /device:TPU:0, one launch (start us, length us, event | category | flops | bytes accessed | tf_op | source)
XLA Modules:
  0.0 168.9 jit_solution(7797106632443361147)
XLA Ops:
  0.6 0.0 copy-start.1
  0.6 0.8 convert_element_type.3
  1.5 1.2 broadcast_multiply_fusion.refs_0_
  2.7 3.1 %collective-permute-start = (bf16[128,3584]{1,0:T(8,128)(2,1)S(1)}, bf16[128,3584]{1,0:T(8,128)(2,1)S(1)}, u32[]{:S(2)}, u32[]{:S(2)}) collective-permute-start(bf16[128,3584]{1,0:T(8,128)(2,1)S(1)} %broadcast_multiply_fusion.refs_0_), channel_id=1, source_target_pairs={{0,1},{1,0},{2,3},{3,2},{4,5},{5,4},{6,7},{7,6},{8,9},{9,8},{10,11... | collective-permute-start | bytes 2752520 | tf_op jit(solution)/shard_map/ppermute | solution.py:448
  5.8 1.2 dynamic_slice.9
  7.0 0.6 pad_bitcast_fusion.flips_ref
  7.7 18.5 %collective-permute-done.refs_1_ = bf16[128,3584]{1,0:T(8,128)(2,1)S(1)} collective-permute-done((bf16[128,3584]{1,0:T(8,128)(2,1)S(1)}, bf16[128,3584]{1,0:T(8,128)(2,1)S(1)}, u32[]{:S(2)}, u32[]{:S(2)}) %collective-permute-start) | collective-permute-done | bytes 917536 | tf_op jit(solution)/shard_map/ppermute | solution.py:448
  26.1 0.0 copy-done.1
  26.1 0.0 copy-start.2
  26.1 1.4 copy-done.2
  27.6 5.6 %rotate.1 = (bf16[128,3584]{1,0:T(8,128)(2,1)S(1)}, f32[8,128]{1,0:T(8,128)S(1)}) custom-call(bf16[896,896]{1,0:T(8,128)(2,1)S(1)} %copy-done.2, bf16[896,896]{1,0:T(8,128)(2,1)S(1)} %copy-done.1, f32[1,2]{1,0:T(1,128)S(1)} %pad_bitcast_fusion.flips_ref, bf16[128,3584]{1,0:T(8,128)(2,1)S(1)} %broadcast_multiply_fusion.refs_0_, ...), custom_call_target="tpu_custom_call" | custom-call | tf_op jit(solution)/shard_map/rotate/pallas_call | solution.py:76
  33.2 97.3 %gather.1 = (bf16[2048,3584]{1,0:T(8,128)(2,1)S(1)}, bf16[2048,512]{1,0:T(8,128)(2,1)S(1)}, f32[32,8,128]{2,1,0:T(8,128)S(1)}) custom-call(bf16[128,3584]{1,0:T(8,128)(2,1)S(1)} %get-tuple-element.10.rot, f32[8,128]{1,0:T(8,128)S(1)} %get-tuple-element.11.part), custom_call_target="tpu_custom_call" | custom-call | tf_op jit(solution)/shard_map/gather/pallas_call | solution.py:329
  130.5 0.0 copy-start
  130.5 5.2 %copy-done = bf16[2048,3584]{1,0:T(8,128)(2,1)} copy-done((bf16[2048,3584]{1,0:T(8,128)(2,1)}, bf16[2048,3584]{1,0:T(8,128)(2,1)S(1)}, u32[]{:S(2)}) %copy-start) | copy-done | bytes 14680088
  135.7 0.6 slice_reduce_fusion.2
  137.1 16.1 %gram.1 = (f32[448,3584]{1,0:T(8,128)}, f32[8,448]{1,0:T(8,128)S(1)}) custom-call(f32[1,1]{1,0:T(1,128)} %bitcast.1.scale_ref, bf16[2048,512]{1,0:T(8,128)(2,1)S(1)} %get-tuple-element.13.window_ref, bf16[2048,3584]{1,0:T(8,128)(2,1)} %copy-done, bf16[2048,3584]{1,0:T(8,128)(2,1)} %copy-done), custom_call_target="tpu_custom_call" | custom-call | flops 6576668672 | bytes 21102592 | tf_op jit(solution)/shard_map/gram/pallas_call | solution.py:406
  153.2 0.0 copy-start.3
  153.2 0.6 copy-done.3
  153.8 12.3 %spread.1 = f32[32,8,448]{2,1,0:T(8,128)} custom-call(f32[8,448]{1,0:T(8,128)} %copy-done.3), custom_call_target="tpu_custom_call" | custom-call | tf_op jit(solution)/shard_map/spread/pallas_call | solution.py:150
  166.1 1.8 %slice_reduce_fusion = (f32[]{:T(128)}, f32[32,448]{1,0:T(8,128)S(1)}) fusion(f32[32,8,448]{2,1,0:T(8,128)} %spread.1), kind=kLoop, calls=%fused_computation.1 | loop fusion | flops 14335 | bytes 114692 | tf_op jit(solution)/shard_map/reduce_max | solution.py:462
  168.0 0.1 reduce_max.18
  168.1 0.1 reshape.18
  168.2 0.7 dynamic_slice.11
  (1 shorter events, 0.0 us)
Async XLA Ops:
  0.6 25.5 %copy-start.1 = (bf16[896,896]{1,0:T(8,128)(2,1)S(1)}, bf16[896,896]{1,0:T(8,128)(2,1)}, u32[]{:S(2)}) copy-start(bf16[896,896]{1,0:T(8,128)(2,1)} %constant.34.clone.low_ref) | copy-start | bytes 4816900
  2.7 23.4 %collective-permute-start = (bf16[128,3584]{1,0:T(8,128)(2,1)S(1)}, bf16[128,3584]{1,0:T(8,128)(2,1)S(1)}, u32[]{:S(2)}, u32[]{:S(2)}) collective-permute-start(bf16[128,3584]{1,0:T(8,128)(2,1)S(1)} %broadcast_multiply_fusion.refs_0_), channel_id=1, source_target_pairs={{0,1},{1,0},{2,3},{3,2},{4,5},{5,4},{6,7},{7,6},{8,9},{9,8},{10,11... | collective-permute-start | bytes 2752520 | tf_op jit(solution)/shard_map/ppermute | solution.py:448
  26.1 1.4 copy-start.2
  130.5 5.2 %copy-start = (bf16[2048,3584]{1,0:T(8,128)(2,1)}, bf16[2048,3584]{1,0:T(8,128)(2,1)S(1)}, u32[]{:S(2)}) copy-start(bf16[2048,3584]{1,0:T(8,128)(2,1)S(1)} %get-tuple-element.14.all_ref.columns_ref) | copy-start | bytes 44040196
  153.2 0.6 copy-start.3
where the time goes:
time: 172 us; the launch traced here: 169 us
  Pallas kernels  131 us (76%)
  waiting for transfers between devices  18.5 us (11%)
  local copies, waits for them, and re-layouts  9.92 us (6%)
  other arithmetic  4.64 us (3%)
  starting transfers between devices  3.06 us (2%)
    pallas_call x1, Pallas kernels, gather(): pl.pallas_call(functools.partial(gather_kernel, depth, across, sub, 1, ro...  97.3 us
    ppermute x1, waiting for transfers between devices, per_device(): piece = lax.ppermute(signed, 'blk', [(i, i ^ k) for i in range(blocks)])  18.5 us
    pallas_call x1, Pallas kernels, gram(): pl.pallas_call(functools.partial(gram_kernel, rows), grid=(width // tile,...  16.1 us
    pallas_call x1, Pallas kernels, spread(): pl.pallas_call(spread_kernel, out_shape=jax.ShapeDtypeStruct((count,) + b...  12.3 us
    unnamed x8, local copies, waits for them, and re-layouts  7.23 us
    pallas_call x1, Pallas kernels, rotate(): pl.pallas_call(functools.partial(rotate_kernel, blocks, width // UNIT), o...  5.62 us
  transfers between devices with their start and end apart: 1, of which 1 were waited for; matrix products, arithmetic and copies ran while one was open for 1% of the time, Pallas kernels for 0%

commit v1 on v0

v1 whole, which is shorter than its diff:
```python
import functools
import math

import jax
import jax.numpy as jnp
import numpy as np
from jax import lax
from jax.experimental import pallas as pl
from jax.experimental.pallas import tpu as pltpu
from jax.sharding import PartitionSpec as P

WALSH = 512
MIX = 14
FEATURES = 7168

EPS = 1e-06
DAMP = 0.01

LANES = 128
UNIT_WALSH = LANES // math.gcd(LANES, MIX)
UNIT = UNIT_WALSH * MIX
MESH = pl.DeviceIdType.MESH


def parity(number):
    return bin(number).count("1") & 1


def unit_tables():
    walsh = np.array(
        [[1 - 2 * parity(i & j) for j in range(UNIT_WALSH)] for i in range(UNIT_WALSH)], np.float64
    )
    k = np.arange(MIX)[:, None]
    n = np.arange(MIX)[None, :]
    cosine = math.sqrt(2.0 / MIX) * np.cos(math.pi * (n + 0.5) * k / MIX)
    cosine[0] *= math.sqrt(0.5)
    table = np.kron(walsh, cosine.T).astype(np.float32)
    high = table.astype(jnp.bfloat16)
    low = (table - high.astype(np.float32)).astype(jnp.bfloat16)
    return high, low


def bits_of(number, count):
    return [number // 2**j % 2 for j in range(count.bit_length() - 1)]


def swapped(me, k, count):
    total = 0
    for j, bit in enumerate(bits_of(me, count)):
        total += ((1 - bit) if k >> j & 1 else bit) * 2**j
    return total


def flip(me, k, count):
    odd = 0
    for j, bit in enumerate(bits_of(me, count)):
        odd += 0 if k >> j & 1 else bit
    return 1.0 if isinstance(odd, int) else (1 - 2 * (odd % 2)).astype(jnp.float32)


def place(tok, row_count, width, window):
    first = tok * row_count
    owner = first // width
    offset = first - owner * width
    start = jnp.minimum(offset // LANES * LANES, width - window)
    return owner, start, offset - start


def window_size(groups, row_count, width):
    need = max(i * row_count % width % LANES + row_count for i in range(groups))
    return min(-(-need // LANES) * LANES, width)


def tile_size(width):
    return max(t for t in range(LANES, 513, LANES) if width % t == 0)


def remote(src, dst, send, arrive, to_tok, to_blk):
    return pltpu.make_async_remote_copy(
        src, dst, send, arrive, device_id={"tok": to_tok, "blk": to_blk}, device_id_type=MESH
    )


def greet_all(tok, blk):
    tokens, blocks = lax.axis_size("tok"), lax.axis_size("blk")
    count = tokens * blocks
    barrier = pltpu.get_barrier_semaphore()
    me = tok * blocks + blk

    @pl.loop(1, count)
    def _(k):
        other = lax.rem(me + k, count)
        pl.semaphore_signal(
            barrier, inc=1, device_id={"tok": other // blocks, "blk": other % blocks}, device_id_type=MESH
        )

    pl.semaphore_wait(barrier, count - 1)


def broadcast_start(tok, blk, src, dst, send, recv):
    tokens, blocks = lax.axis_size("tok"), lax.axis_size("blk")
    count = tokens * blocks
    me = tok * blocks + blk

    @pl.loop(1, count)
    def _(k):
        other = lax.rem(me + k, count)
        remote(src, dst.at[me], send, recv, other // blocks, other % blocks).start()


def broadcast_wait(tok, blk, dst, send, recv):
    count = lax.axis_size("tok") * lax.axis_size("blk") - 1
    both = remote(dst.at[pl.ds(0, count)], dst.at[pl.ds(0, count)], send, recv, tok, blk)
    both.wait_send()
    both.wait_recv()


def kernel(
    depth, across, sub, early, lag, row_count, x_ref, signs_ref, high_hbm, low_hbm,
    hess_ref, ratio_ref, top_ref,
    cols, rows, pieces, signs, high, low, lhs, acc, left, square, parts, best, peaks,
    table_sem, x_sem, sign_sem, sign_send, sign_recv, swap_send, swap_recv,
    recv, pair_send, pair_recv, z_send, x_send, y_send, y_recv, part_send, part_recv, peak_send, peak_recv,
):
    tok, blk = lax.axis_index("tok"), lax.axis_index("blk")
    blocks, groups = lax.axis_size("blk"), lax.axis_size("tok")
    tok_rows, width = x_ref.shape
    window = rows.shape[1]
    half = cols.shape[0] // 2
    steps = tok_rows // sub
    chunks = width // UNIT
    core, chip = tok % 2, tok // 2
    z, x = chip // across, chip % across
    me = tok * blocks + blk
    owner, start, skew = place(tok, row_count, width, window)
    start = pl.multiple_of(start, LANES)

    loads = [
        pltpu.make_async_copy(high_hbm, high, table_sem.at[0]),
        pltpu.make_async_copy(low_hbm, low, table_sem.at[1]),
        pltpu.make_async_copy(x_ref, pieces.at[0], x_sem),
        pltpu.make_async_copy(signs_ref, signs.at[0], sign_sem),
    ]
    for load in loads:
        load.start()
    greet_all(tok, blk)

    for k in range(1, blocks):
        remote(signs_ref, signs.at[k], sign_send, sign_recv.at[k], tok, swapped(blk, k, blocks)).start()

    @pl.loop(0, steps)
    def _(s):
        piece = pl.ds(pl.multiple_of(s * sub, sub), sub)
        for k in range(1, blocks):
            remote(
                x_ref.at[piece], pieces.at[k, piece], swap_send, swap_recv.at[k * steps + s],
                tok, swapped(blk, k, blocks),
            ).start()

    for load in loads:
        load.wait()
    for k in range(1, blocks):
        remote(signs.at[k], signs.at[k], sign_send, sign_recv.at[k], tok, blk).wait_recv()
    square[...] = jnp.zeros_like(square)

    def first_row(oz, ox, s):
        return pl.multiple_of(((oz * across + ox) * 2 + core) * tok_rows + s * sub, sub)

    def rotate(s):
        piece = pl.ds(pl.multiple_of(s * sub, sub), sub)
        for k in range(1, blocks):
            landed = pieces.at[k, piece]
            remote(landed, landed, swap_send, swap_recv.at[k * steps + s], tok, blk).wait_recv()
        for k in range(blocks):
            for c in range(chunks):
                lanes = slice(c * UNIT, (c + 1) * UNIT)
                value = pieces[k, piece, lanes].astype(jnp.float32) * signs[k, :, lanes]
                first = (k * chunks + c) * sub
                lhs[first : first + sub, :] = value.astype(jnp.bfloat16)
        value = jnp.dot(lhs[...], high[...], preferred_element_type=jnp.float32)
        value += jnp.dot(lhs[...], low[...], preferred_element_type=jnp.float32)
        mixed = []
        for c in range(chunks):
            total = None
            for k in range(blocks):
                first = (k * chunks + c) * sub
                part = value[first : first + sub] * flip(blk, k, blocks)
                total = part if total is None else total + part
            mixed.append(total)
        step = 1
        while step < chunks:
            for a in range(chunks):
                if not a & step:
                    p, q = mixed[a], mixed[a | step]
                    mixed[a], mixed[a | step] = p + q, p - q
            step *= 2
        row = first_row(z, x, s)
        total = square[...]
        for c in range(chunks):
            rounded = (mixed[c] * (1.0 / math.sqrt(WALSH))).astype(jnp.bfloat16)
            cols[pl.ds(row, sub), c * UNIT : (c + 1) * UNIT] = rounded
            wide = rounded.astype(jnp.float32)
            wide = wide * wide
            for i in range(0, sub, 8):
                for j in range(0, UNIT, LANES):
                    total += wide[i : i + 8, j : j + LANES]
        square[...] = total

    def fan(oz, ox, s, z_ways, x_ways):
        row = first_row(oz, ox, s)
        src = cols.at[pl.ds(row, sub)]
        arrive = recv.at[(oz * across + ox) * steps + s]
        for way in z_ways:

            @pl.when((z + way >= 0) & (z + way < depth))
            def _():
                remote(src, src, z_send.at[(way + 1) // 2], arrive, tok + 2 * across * way, blk).start()

        for way in x_ways:

            @pl.when((x + way >= 0) & (x + way < across))
            def _():
                remote(src, src, x_send.at[(way + 1) // 2], arrive, tok + 2 * way, blk).start()

        remote(src, src, pair_send, pair_recv.at[oz * across + ox], tok + 1 - 2 * core, blk).start()
        for j in range(2):
            j_owner, j_start, _ = place(chip * 2 + j, row_count, width, window)

            @pl.when(j_owner == blk)
            def _():
                part = cols.at[pl.ds(row, sub), pl.ds(pl.multiple_of(j_start, LANES), window)]
                for k in range(1, blocks):
                    remote(
                        part, rows.at[pl.ds(row, sub)], y_send.at[2 * k + j],
                        y_recv.at[oz * across + ox], chip * 2 + j, lax.rem(blk + k, blocks),
                    ).start()

    def relay(oz, ox, s, z_ways, x_ways):
        piece = cols.at[pl.ds(first_row(oz, ox, s), sub)]
        remote(piece, piece, pair_send, recv.at[(oz * across + ox) * steps + s], tok, blk).wait_recv()
        fan(oz, ox, s, z_ways, x_ways)

    def inside(oz, ox):
        return (oz >= 0) & (oz < depth) & (ox >= 0) & (ox < across)

    def along_z(d, s):
        for way in (1, -1):
            oz = z - way * d

            @pl.when(inside(oz, x))
            def _():
                relay(oz, x, s, (way,), (1, -1))

    def along_x(d, dx, s):
        for side in (1, -1) if d else (1,):
            oz = z - side * d
            for way in (1, -1):
                ox = x - way * dx

                @pl.when(inside(oz, ox))
                def _():
                    relay(oz, ox, s, (), (way,))

    def early_x(dx, s):
        for way in (1, -1):
            ox = x - way * dx

            @pl.when(inside(z, ox))
            def _():
                relay(z, ox, s, (1, -1), (way,))

    def early_z(d):
        for way in (1, -1):
            oz = z - way * d

            @pl.when(inside(oz, x))
            def _():
                @pl.loop(0, across * early)
                def _(n):
                    relay(oz, n // early, n % early, (way,), ())

    tile = tile_size(width)

    def gram(stage):
        @pl.loop(0, depth * across)
        def _(n):
            oz, ox = n // across, n % across

            def away(a, b, d):
                return (a - b == d) | (b - a == d)

            due = (ox == x) & away(oz, z, stage)
            if stage:
                due = due | away(ox, x, 1) & away(oz, z, stage - 1)
            if stage == depth:
                for dx in range(2, across):
                    due = due | away(ox, x, dx)

            @pl.when(due)
            def _():
                chunk = pl.ds(pl.multiple_of(n * 2 * tok_rows, sub), 2 * tok_rows)
                piece = cols.at[pl.ds(0, tok_rows)]
                remote(piece, piece, pair_send, pair_recv.at[n], tok, blk).wait_recv()

                @pl.when(owner == blk)
                def _():
                    left[...] = jnp.transpose(cols[chunk, pl.ds(start, window)])

                @pl.when(owner != blk)
                def _():
                    piece = rows.at[pl.ds(0, 2 * tok_rows)]
                    remote(piece, piece, pair_send, y_recv.at[n], tok, blk).wait_recv()
                    left[...] = jnp.transpose(rows[chunk, :])

                @pl.loop(0, width // tile)
                def _(t):
                    lanes = pl.ds(pl.multiple_of(t * tile, tile), tile)
                    block = jnp.dot(left[...], cols[chunk, lanes], preferred_element_type=jnp.float32)
                    if stage:
                        acc[:, lanes] += block
                    else:
                        acc[:, lanes] = block

    @pl.loop(0, steps + lag)
    def _(s):
        @pl.when(s < steps)
        def _():
            rotate(s)
            fan(z, x, s, (1, -1), (1, -1))

        if depth * across > 1:

            @pl.when((s >= lag) & (s < lag + early))
            def _():
                for dx in range(1, across):
                    early_x(dx, s - lag)

            @pl.when(s >= lag + early)
            def _():
                along_z(1, s - lag)
                along_x(0, 1, s - lag)

    parts[me] = square[...]
    broadcast_start(tok, blk, square, parts, part_send, part_recv)
    gram(0)
    early_z(1)
    for d in range(2, depth):

        @pl.loop(early, steps)
        def _(s):
            along_z(d, s)
            along_x(d - 1, 1, s)

        early_z(d)
        gram(d - 1)

    @pl.loop(early, steps)
    def _(s):
        along_x(depth - 1, 1, s)

    for dx in range(2, across):
        for d in range(depth):

            @pl.loop(early, steps)
            def _(s):
                along_x(d, dx, s)

    gram(depth - 1)
    gram(depth)

    broadcast_wait(tok, blk, parts, part_send, part_recv)
    total = jnp.sum(jnp.sum(parts[...], axis=0), keepdims=True)
    inverse = 1.0 / (total / FEATURES + EPS)
    base = tok * row_count - blk * width

    best[...] = jnp.zeros_like(best)

    @pl.loop(0, width // tile)
    def _(t):
        lanes = pl.ds(pl.multiple_of(t * tile, tile), tile)
        row = lax.broadcasted_iota(jnp.int32, (window, tile), 0) + (base - skew - t * tile)
        column = lax.broadcasted_iota(jnp.int32, (window, tile), 1)
        size = jnp.where(row == column, 0.0, jnp.abs(acc[:, lanes]))
        most = best[...]
        for j in range(0, tile, LANES):
            most = jnp.maximum(most, size[:, j : j + LANES])
        best[...] = most

    flat = jnp.max(jnp.transpose(best[...]), axis=0, keepdims=True)
    lane = lax.broadcasted_iota(jnp.int32, (1, window), 1)
    flat = jnp.where((lane >= skew) & (lane < skew + row_count), flat, 0.0) * inverse
    peaks[me] = flat
    broadcast_start(tok, blk, peaks.at[me], peaks, peak_send, peak_recv)

    @pl.loop(0, width // tile)
    def _(t):
        lanes = pl.ds(pl.multiple_of(t * tile, tile), tile)
        row = lax.broadcasted_iota(jnp.int32, (row_count, tile), 0) + (base - t * tile)
        column = lax.broadcasted_iota(jnp.int32, (row_count, tile), 1)
        block = acc[pl.ds(pl.multiple_of(skew, 8), row_count), lanes]
        hess_ref[:, lanes] = block * inverse + jnp.where(row == column, DAMP, 0.0)

    def settle(count, send):
        piece = cols.at[pl.ds(0, count)]
        remote(piece, piece, send, part_recv, tok, blk).wait_send()

    late = steps - early
    for v in range(depth):

        @pl.when(z == v)
        def _():
            unit = (late + early * across) * sub
            if v < depth - 1:
                settle((v + 1) * unit, z_send.at[1])
            if v > 0:
                settle((depth - v) * unit, z_send.at[0])

    for v in range(across):

        @pl.when(x == v)
        def _():
            unit = (late * depth + early) * sub
            if v < across - 1:
                settle((v + 1) * unit, x_send.at[1])
            if v > 0:
                settle((across - v) * unit, x_send.at[0])

    settle(half, pair_send)
    for j in range(2):
        j_owner, _, _ = place(chip * 2 + j, row_count, width, window)

        @pl.when(j_owner == blk)
        def _():
            piece = rows.at[pl.ds(0, half)]
            for k in range(1, blocks):
                remote(piece, piece, y_send.at[2 * k + j], part_recv, tok, blk).wait_send()

    for k in range(1, blocks):
        remote(signs.at[k], signs.at[k], sign_send, part_recv, tok, blk).wait_send()
    if blocks > 1:
        sent = pieces.at[pl.ds(0, blocks - 1)]
        remote(sent, sent, swap_send, part_recv, tok, blk).wait_send()

    broadcast_wait(tok, blk, peaks, peak_send, peak_recv)
    most = peaks[0]
    for i in range(1, groups * blocks):
        most = jnp.maximum(most, peaks[i])
    top_ref[...] = jnp.broadcast_to(jnp.max(most, keepdims=True), top_ref.shape)
    for j in range(0, width, window):
        ratio_ref[:, j : j + window] = jnp.zeros((1, window), jnp.float32)
    for b in range(blocks):

        @pl.when(blk == b)
        def _():
            for i in range(groups):
                first = i * row_count
                if first // width == b:
                    offset = first % width
                    begin = min(offset // LANES * LANES, width - window)
                    most = ratio_ref[:, begin : begin + window]
                    for k in range(blocks):
                        most = jnp.maximum(most, peaks[i * blocks + k])
                    ratio_ref[:, begin : begin + window] = most


def per_device(activations, signs):
    tok_rows, width = activations.shape
    groups, blocks = lax.axis_size("tok"), lax.axis_size("blk")
    depth = 4 if groups % 8 == 0 else 1
    across = groups // (2 * depth)
    sub, early, lag = 16, 1, 2
    steps = tok_rows // sub
    row_count = FEATURES // groups
    window = window_size(groups, row_count, width)
    count, chips, tokens = groups * blocks, groups // 2, groups * tok_rows
    high, low = unit_tables()
    dma = pltpu.SemaphoreType.DMA
    anywhere = pl.BlockSpec(memory_space=pl.ANY)
    vmem = pl.BlockSpec(memory_space=pltpu.VMEM)
    hessian, ratio, top = pl.pallas_call(
        functools.partial(kernel, depth, across, sub, early, lag, row_count),
        out_shape=(
            jax.ShapeDtypeStruct((row_count, width), jnp.float32),
            jax.ShapeDtypeStruct((1, width + window), jnp.float32),
            jax.ShapeDtypeStruct((8, LANES), jnp.float32),
        ),
        in_specs=[anywhere] * 4,
        out_specs=(vmem, vmem, vmem),
        scratch_shapes=[
            pltpu.VMEM((tokens, width), jnp.bfloat16),
            pltpu.VMEM((tokens, window), jnp.bfloat16),
            pltpu.VMEM((blocks, tok_rows, width), jnp.bfloat16),
            pltpu.VMEM((blocks + 1, 1, width), jnp.float32),
            pltpu.VMEM((UNIT, UNIT), jnp.bfloat16),
            pltpu.VMEM((UNIT, UNIT), jnp.bfloat16),
            pltpu.VMEM((blocks * (width // UNIT) * sub, UNIT), jnp.bfloat16),
            pltpu.VMEM((window, width), jnp.float32),
            pltpu.VMEM((window, 2 * tok_rows), jnp.bfloat16),
            pltpu.VMEM((8, LANES), jnp.float32),
            pltpu.VMEM((count, 8, LANES), jnp.float32),
            pltpu.VMEM((window, LANES), jnp.float32),
            pltpu.VMEM((count + 1, 1, window), jnp.float32),
            dma((2,)), dma, dma, dma, dma((blocks,)), dma, dma((blocks * steps,)),
            dma((chips * steps,)), dma, dma((chips,)), dma((2,)), dma((2,)), dma((2 * blocks,)), dma((chips,)),
            dma, dma, dma, dma,
        ],
        compiler_params=pltpu.CompilerParams(
            collective_id=0, has_side_effects=True, vmem_limit_bytes=56 * 1024 * 1024
        ),
        name="fused",
    )(activations, signs.reshape(1, width), jnp.asarray(high), jnp.asarray(low))
    return hessian, ratio[0, :width], top[0, 0]


def solution(mesh):
    in_specs = (P("tok", "blk"), P("blk"))
    out_specs = (P("tok", "blk"), P("blk"), P())
    return jax.shard_map(
        per_device, mesh=mesh, in_specs=in_specs, out_specs=out_specs, check_vma=False
    )
```

time: 172 us -> 118 us (0.69); the launches traced: 169 us -> 118 us
  Pallas kernels: 131 us -> 107 us
  waiting for transfers between devices: 18.5 us -> 0 us
  other arithmetic: 4.64 us -> 0 us
  starting transfers between devices: 3.06 us -> 0 us
    pallas_call x4 -> x1, Pallas kernels: 131 us -> 107 us  [per_device(): pl.pallas_call(functools.partial(kernel, depth, across, sub, early, lag,...]
    ppermute x1 -> x0, waiting for transfers between devices: 18.5 us -> none  [per_device(): piece = lax.ppermute(signed, 'blk', [(i, i ^ k) for i in range(blocks)])]
    ppermute x1 -> x0, starting transfers between devices: 3.06 us -> none  [per_device(): piece = lax.ppermute(signed, 'blk', [(i, i ^ k) for i in range(blocks)])]
    slice x0 -> x2, local copies, waits for them, and re-layouts: none -> 2.54 us  [per_device(): return (hessian, ratio[0, :width], top[0, 0])]
    reduce_max x2 -> x0, other arithmetic: 1.92 us -> none  [the longest x1 1.85 us: per_device(): return (hessian, incoherence, jnp.max(ratios))]
    dynamic_slice x2 -> x0, local copies, waits for them, and re-layouts: 1.92 us -> none  [the longest x1 1.24 us: per_device(): flips.append(table[me])]
    unnamed x8 -> x1, local copies, waits for them, and re-layouts: 7.23 us -> 5.99 us
  transfers between devices with their start and end apart: 1 -> 0, of which waited for: 1 -> 0; matrix products, arithmetic and copies ran while one was open for 1% -> 0% of each run, Pallas kernels for 0% -> 0%
where the time goes in v1:
time: 118 us
  Pallas kernels  107 us (91%)
  local copies, waits for them, and re-layouts  9.87 us (8%)
    pallas_call x1, Pallas kernels, per_device(): pl.pallas_call(functools.partial(kernel, depth, across, sub, early, lag,...  107 us
    unnamed x1, local copies, waits for them, and re-layouts  5.99 us
    slice x2, local copies, waits for them, and re-layouts, per_device(): return (hessian, ratio[0, :width], top[0, 0])  2.54 us

profile of v1, /device:TPU:0, one launch (start us, length us, event | category | flops | bytes accessed | tf_op | source)
XLA Modules:
  0.0 118.0 jit_solution(11706015862056574861)
XLA Ops:
  0.6 1.3 %reshape.9.signs_ref = f32[1,3584]{1,0:T(1,128)} reshape(f32[3584]{0:T(1024)} %param.5) | data formatting | bytes 28672 | tf_op jit(solution)/shard_map/reshape | solution.py:511
  2.0 107.5 %fused.1 = (f32[448,3584]{1,0:T(8,128)}, f32[1,4096]{1,0:T(1,128)}, f32[8,128]{1,0:T(8,128)}) custom-call(bf16[128,3584]{1,0:T(8,128)(2,1)} %x_ref.1, f32[1,3584]{1,0:T(1,128)} %reshape.9.signs_ref, bf16[896,896]{1,0:T(8,128)(2,1)} %constant.4.clone.high_hbm, bf16[896,896]{1,0:T(8,128)(2,1)} %constant.5.clone.low_hbm), custom_call_target="tpu_custom_call" | custom-call | tf_op jit(solution)/shard_map/fused/pallas_call | solution.py:480
  109.4 1.2 %slice.7 = f32[1,1]{1,0:T(1,128)} slice(f32[8,128]{1,0:T(8,128)} %get-tuple-element.8), slice={[0:1], [0:1]} | slice | bytes 8 | tf_op jit(solution)/shard_map/slice | solution.py:512
  110.6 1.4 %slice_reduce_fusion = f32[3584]{0:T(1024)} fusion(f32[1,4096]{1,0:T(1,128)} %get-tuple-element.7), kind=kLoop, calls=%fused_computation | loop fusion | bytes 28672 | tf_op jit(solution)/shard_map/slice | solution.py:512
  112.0 6.0 %copy.8 = f32[448,3584]{1,0:T(8,128)} copy(f32[448,3584]{1,0:T(8,128)} %get-tuple-element.12) | data formatting | bytes 12845056

commit v2 on v1

--- a/solution.py
+++ b/solution.py
@@ -81,20 +81,30 @@
     )
 
 
-def greet_all(tok, blk):
-    tokens, blocks = lax.axis_size("tok"), lax.axis_size("blk")
-    count = tokens * blocks
+def greet(tok, blk, core, z, x, depth, across):
+    blocks = lax.axis_size("blk")
     barrier = pltpu.get_barrier_semaphore()
-    me = tok * blocks + blk
-
-    @pl.loop(1, count)
-    def _(k):
-        other = lax.rem(me + k, count)
-        pl.semaphore_signal(
-            barrier, inc=1, device_id={"tok": other // blocks, "blk": other % blocks}, device_id_type=MESH
-        )
-
-    pl.semaphore_wait(barrier, count - 1)
+
+    def signal(to_tok, to_blk):
+        pl.semaphore_signal(barrier, inc=1, device_id={"tok": to_tok, "blk": to_blk}, device_id_type=MESH)
+
+    twin = tok + 1 - 2 * core
+    for k in range(1, blocks):
+        other = swapped(blk, k, blocks)
+        signal(tok, other)
+        signal(twin, other)
+    count = 2 * blocks - 1
+    for place_, size, stride in ((x, across, 2), (z, depth, 2 * across)):
+        for way in (1, -1):
+            there = (place_ + way >= 0) & (place_ + way < size)
+            count += there.astype(jnp.int32)
+
+            @pl.when(there)
+            def _():
+                signal(tok + stride * way, blk)
+
+    signal(twin, blk)
+    pl.semaphore_wait(barrier, count)
 
 
 def broadcast_start(tok, blk, src, dst, send, recv):
@@ -117,10 +127,21 @@
 
 def kernel(
     depth, across, sub, early, lag, row_count, x_ref, signs_ref, high_hbm, low_hbm,
-    hess_ref, ratio_ref, top_ref,
-    cols, rows, pieces, signs, high, low, lhs, acc, left, square, parts, best, peaks,
+    acc, notes, cols, rows, pieces, *rest,
+):
+    blocks, width = lax.axis_size("blk"), x_ref.shape[1]
+    signs, rest = [ref.at[pl.ds(0, width)] for ref in rest[:blocks]], rest[blocks:]
+    run(
+        depth, across, sub, early, lag, row_count, x_ref, signs_ref, high_hbm, low_hbm,
+        acc, notes, cols, rows, pieces, signs, *rest,
+    )
+
+
+def run(
+    depth, across, sub, early, lag, row_count, x_ref, signs_ref, high_hbm, low_hbm,
+    acc, notes, cols, rows, pieces, signs, high, low, lhs, left, square, best,
     table_sem, x_sem, sign_sem, sign_send, sign_recv, swap_send, swap_recv,
-    recv, pair_send, pair_recv, z_send, x_send, y_send, y_recv, part_send, part_recv, peak_send, peak_recv,
+    recv, pair_send, pair_recv, z_send, x_send, y_send, y_recv, note_send, note_recv,
 ):
     tok, blk = lax.axis_index("tok"), lax.axis_index("blk")
     blocks, groups = lax.axis_size("blk"), lax.axis_size("tok")
@@ -139,14 +160,14 @@
         pltpu.make_async_copy(high_hbm, high, table_sem.at[0]),
         pltpu.make_async_copy(low_hbm, low, table_sem.at[1]),
         pltpu.make_async_copy(x_ref, pieces.at[0], x_sem),
-        pltpu.make_async_copy(signs_ref, signs.at[0], sign_sem),
+        pltpu.make_async_copy(signs_ref, signs[0], sign_sem),
     ]
     for load in loads:
         load.start()
-    greet_all(tok, blk)
+    greet(tok, blk, core, z, x, depth, across)
 
     for k in range(1, blocks):
-        remote(signs_ref, signs.at[k], sign_send, sign_recv.at[k], tok, swapped(blk, k, blocks)).start()
+        remote(signs_ref, signs[k], sign_send, sign_recv.at[k], tok, swapped(blk, k, blocks)).start()
 
     @pl.loop(0, steps)
     def _(s):
@@ -160,9 +181,7 @@
     for load in loads:
         load.wait()
     for k in range(1, blocks):
-        remote(signs.at[k], signs.at[k], sign_send, sign_recv.at[k], tok, blk).wait_recv()
-    square[...] = jnp.zeros_like(square)
-
+        remote(signs[k], signs[k], sign_send, sign_recv.at[k], tok, blk).wait_recv()
     def first_row(oz, ox, s):
         return pl.multiple_of(((oz * across + ox) * 2 + core) * tok_rows + s * sub, sub)
 
@@ -174,7 +193,7 @@
         for k in range(blocks):
             for c in range(chunks):
                 lanes = slice(c * UNIT, (c + 1) * UNIT)
-                value = pieces[k, piece, lanes].astype(jnp.float32) * signs[k, :, lanes]
+                value = pieces[k, piece, lanes].astype(jnp.float32) * signs[k][lanes].reshape(1, UNIT)
                 first = (k * chunks + c) * sub
                 lhs[first : first + sub, :] = value.astype(jnp.bfloat16)
         value = jnp.dot(lhs[...], high[...], preferred_element_type=jnp.float32)
@@ -247,9 +266,13 @@
         for way in (1, -1):
             oz = z - way * d
 
-            @pl.when(inside(oz, x))
+            @pl.when(inside(oz, x) & (s >= early))
             def _():
                 relay(oz, x, s, (way,), (1, -1))
+
+            @pl.when(inside(oz, x) & (s < early))
+            def _():
+                relay(oz, x, s, (way,), ())
 
     def along_x(d, dx, s):
         for side in (1, -1) if d else (1,):
@@ -269,57 +292,87 @@
             def _():
                 relay(z, ox, s, (1, -1), (way,))
 
-    def early_z(d):
+    def extra_z(d):
         for way in (1, -1):
             oz = z - way * d
-
-            @pl.when(inside(oz, x))
-            def _():
-                @pl.loop(0, across * early)
-                def _(n):
-                    relay(oz, n // early, n % early, (way,), ())
+            for dx in range(1, across):
+                for side in (1, -1):
+                    ox = x - side * dx
+
+                    @pl.when(inside(oz, ox))
+                    def _():
+                        for s in range(early):
+                            relay(oz, ox, s, (way,), ())
 
     tile = tile_size(width)
-
-    def gram(stage):
-        @pl.loop(0, depth * across)
-        def _(n):
-            oz, ox = n // across, n % across
-
-            def away(a, b, d):
-                return (a - b == d) | (b - a == d)
-
-            due = (ox == x) & away(oz, z, stage)
-            if stage:
-                due = due | away(ox, x, 1) & away(oz, z, stage - 1)
-            if stage == depth:
-                for dx in range(2, across):
-                    due = due | away(ox, x, dx)
-
-            @pl.when(due)
-            def _():
-                chunk = pl.ds(pl.multiple_of(n * 2 * tok_rows, sub), 2 * tok_rows)
-                piece = cols.at[pl.ds(0, tok_rows)]
-                remote(piece, piece, pair_send, pair_recv.at[n], tok, blk).wait_recv()
-
-                @pl.when(owner == blk)
-                def _():
-                    left[...] = jnp.transpose(cols[chunk, pl.ds(start, window)])
-
-                @pl.when(owner != blk)
-                def _():
-                    piece = rows.at[pl.ds(0, 2 * tok_rows)]
-                    remote(piece, piece, pair_send, y_recv.at[n], tok, blk).wait_recv()
-                    left[...] = jnp.transpose(rows[chunk, :])
-
-                @pl.loop(0, width // tile)
-                def _(t):
-                    lanes = pl.ds(pl.multiple_of(t * tile, tile), tile)
-                    block = jnp.dot(left[...], cols[chunk, lanes], preferred_element_type=jnp.float32)
-                    if stage:
-                        acc[:, lanes] += block
-                    else:
-                        acc[:, lanes] = block
+    tiles = width // tile
+    chunks_all = depth * across
+    base = tok * row_count - blk * width - skew
+
+    def chunk_at(q):
+        k, ox = q // across, lax.rem(x + q % across, across)
+        if depth == 1:
+            return k, ox
+        near = z < depth // 2
+        edge = jnp.where(near, z, depth - 1 - z)
+        oz = jnp.where(k == 0, edge, jnp.where(k == 1, 1 - edge, k))
+        return jnp.where(near, oz, depth - 1 - oz), ox
+
+    def gram_open(q):
+        oz, ox = chunk_at(q)
+        n = oz * across + ox
+        chunk = pl.ds(pl.multiple_of(n * 2 * tok_rows, sub), 2 * tok_rows)
+        piece = cols.at[pl.ds(0, tok_rows)]
+        remote(piece, piece, pair_send, pair_recv.at[n], tok, blk).wait_recv()
+
+        @pl.when(owner == blk)
+        def _():
+            left[...] = jnp.transpose(cols[chunk, pl.ds(start, window)])
+
+        @pl.when(owner != blk)
+        def _():
+            piece = rows.at[pl.ds(0, 2 * tok_rows)]
+            remote(piece, piece, pair_send, y_recv.at[n], tok, blk).wait_recv()
+            left[...] = jnp.transpose(rows[chunk, :])
+
+    def gram_tile(q, t, first, last):
+        oz, ox = chunk_at(q)
+        n = oz * across + ox
+        chunk = pl.ds(pl.multiple_of(n * 2 * tok_rows, sub), 2 * tok_rows)
+        lanes = pl.ds(pl.multiple_of(t * tile, tile), tile)
+        block = jnp.dot(left[...], cols[chunk, lanes], preferred_element_type=jnp.float32)
+        if not first:
+            block += acc[:, lanes]
+        acc[:, lanes] = block
+        if last:
+            row = lax.broadcasted_iota(jnp.int32, (window, tile), 0) + (base - t * tile)
+            column = lax.broadcasted_iota(jnp.int32, (window, tile), 1)
+            size = jnp.where(row == column, 0.0, jnp.abs(block))
+            most = best[...]
+            for j in range(0, tile, LANES):
+                most = jnp.maximum(most, size[:, j : j + LANES])
+            best[...] = most
+
+    def gram_whole(q, first=False, last=False):
+        gram_open(q)
+
+        @pl.loop(0, tiles)
+        def _(t):
+            gram_tile(q, t, first, last)
+
+    def gram_some(begin, count):
+        @pl.loop(begin, begin + count)
+        def _(g):
+            q, t = g // tiles, g % tiles
+
+            @pl.when(t == 0)
+            def _():
+                gram_open(q)
+
+            gram_tile(q, t, False, False)
+
+    square[...] = jnp.zeros_like(square)
+    best[...] = jnp.zeros_like(best)
 
     @pl.loop(0, steps + lag)
     def _(s):
@@ -328,35 +381,50 @@
             rotate(s)
             fan(z, x, s, (1, -1), (1, -1))
 
-        if depth * across > 1:
-
-            @pl.when((s >= lag) & (s < lag + early))
+        u = s - lag
+        if depth > 1:
+
+            @pl.when(u >= 0)
+            def _():
+                along_z(1, u)
+
+        if across > 1:
+
+            @pl.when((u >= 0) & (u < early))
             def _():
                 for dx in range(1, across):
-                    early_x(dx, s - lag)
-
-            @pl.when(s >= lag + early)
-            def _():
-                along_z(1, s - lag)
-                along_x(0, 1, s - lag)
-
-    parts[me] = square[...]
-    broadcast_start(tok, blk, square, parts, part_send, part_recv)
-    gram(0)
-    early_z(1)
-    for d in range(2, depth):
-
-        @pl.loop(early, steps)
+                    early_x(dx, u)
+
+            @pl.when(u >= early)
+            def _():
+                along_x(0, 1, u)
+
+    extra_z(1)
+    gram_whole(0, first=True)
+    done = tiles
+    paced = across == 2 and depth == 4
+    ready = {2: 3, 3: 5, 4: 7}
+    for d in range(2, depth + 1):
+        goal = ready[d] * tiles if paced else done
+        per = -(-(goal - done) // steps)
+
+        @pl.loop(0, steps)
         def _(s):
-            along_z(d, s)
-            along_x(d - 1, 1, s)
-
-        early_z(d)
-        gram(d - 1)
-
-    @pl.loop(early, steps)
-    def _(s):
-        along_x(depth - 1, 1, s)
+            if d < depth:
+                along_z(d, s)
+            if across > 1:
+
+                @pl.when(s >= early)
+                def _():
+                    along_x(d - 1, 1, s)
+
+            if paced:
+                begin = jnp.minimum(done + s * per, goal)
+                gram_some(begin, jnp.minimum(per, goal - begin))
+
+        if d < depth:
+            extra_z(d)
+        done = goal
 
     for dx in range(2, across):
         for d in range(depth):
@@ -365,44 +433,18 @@
             def _(s):
                 along_x(d, dx, s)
 
-    gram(depth - 1)
-    gram(depth)
-
-    broadcast_wait(tok, blk, parts, part_send, part_recv)
-    total = jnp.sum(jnp.sum(parts[...], axis=0), keepdims=True)
-    inverse = 1.0 / (total / FEATURES + EPS)
-    base = tok * row_count - blk * width
-
-    best[...] = jnp.zeros_like(best)
-
-    @pl.loop(0, width // tile)
-    def _(t):
-        lanes = pl.ds(pl.multiple_of(t * tile, tile), tile)
-        row = lax.broadcasted_iota(jnp.int32, (window, tile), 0) + (base - skew - t * tile)
-        column = lax.broadcasted_iota(jnp.int32, (window, tile), 1)
-        size = jnp.where(row == column, 0.0, jnp.abs(acc[:, lanes]))
-        most = best[...]
-        for j in range(0, tile, LANES):
-            most = jnp.maximum(most, size[:, j : j + LANES])
-        best[...] = most
+    gram_some(done, (chunks_all - 1) * tiles - done)
+    gram_whole(chunks_all - 1, last=True)
 
     flat = jnp.max(jnp.transpose(best[...]), axis=0, keepdims=True)
     lane = lax.broadcasted_iota(jnp.int32, (1, window), 1)
-    flat = jnp.where((lane >= skew) & (lane < skew + row_count), flat, 0.0) * inverse
-    peaks[me] = flat
-    broadcast_start(tok, blk, peaks.at[me], peaks, peak_send, peak_recv)
-
-    @pl.loop(0, width // tile)
-    def _(t):
-        lanes = pl.ds(pl.multiple_of(t * tile, tile), tile)
-        row = lax.broadcasted_iota(jnp.int32, (row_count, tile), 0) + (base - t * tile)
-        column = lax.broadcasted_iota(jnp.int32, (row_count, tile), 1)
-        block = acc[pl.ds(pl.multiple_of(skew, 8), row_count), lanes]
-        hess_ref[:, lanes] = block * inverse + jnp.where(row == column, DAMP, 0.0)
+    notes[me, :, :window] = jnp.where((lane >= skew) & (lane < skew + row_count), flat, 0.0)
+    notes[me, :, window:] = jnp.sum(square[...], axis=0, keepdims=True)
+    broadcast_start(tok, blk, notes.at[me], notes, note_send, note_recv)
 
     def settle(count, send):
         piece = cols.at[pl.ds(0, count)]
-        remote(piece, piece, send, part_recv, tok, blk).wait_send()
+        remote(piece, piece, send, note_recv, tok, blk).wait_send()
 
     late = steps - early
     for v in range(depth):
@@ -433,34 +475,61 @@
         def _():
             piece = rows.at[pl.ds(0, half)]
             for k in range(1, blocks):
-                remote(piece, piece, y_send.at[2 * k + j], part_recv, tok, blk).wait_send()
+                remote(piece, piece, y_send.at[2 * k + j], note_recv, tok, blk).wait_send()
 
     for k in range(1, blocks):
-        remote(signs.at[k], signs.at[k], sign_send, part_recv, tok, blk).wait_send()
+        remote(signs[k], signs[k], sign_send, note_recv, tok, blk).wait_send()
     if blocks > 1:
         sent = pieces.at[pl.ds(0, blocks - 1)]
-        remote(sent, sent, swap_send, part_recv, tok, blk).wait_send()
-
-    broadcast_wait(tok, blk, peaks, peak_send, peak_recv)
-    most = peaks[0]
+        remote(sent, sent, swap_send, note_recv, tok, blk).wait_send()
+
+    broadcast_wait(tok, blk, notes, note_send, note_recv)
+
+
+def finish_kernel(row_count, lines, acc, notes, hess_ref, ratio_ref, top_ref, scaled, sems):
+    tok, blk = lax.axis_index("tok"), lax.axis_index("blk")
+    blocks, groups = lax.axis_size("blk"), lax.axis_size("tok")
+    window, width = acc.shape
+    _, _, skew = place(tok, row_count, width, window)
+    total, most = notes[0, :, window:], notes[0, :, :window]
     for i in range(1, groups * blocks):
-        most = jnp.maximum(most, peaks[i])
-    top_ref[...] = jnp.broadcast_to(jnp.max(most, keepdims=True), top_ref.shape)
-    for j in range(0, width, window):
-        ratio_ref[:, j : j + window] = jnp.zeros((1, window), jnp.float32)
+        total += notes[i, :, window:]
+        most = jnp.maximum(most, notes[i, :, :window])
+    inverse = 1.0 / (jnp.sum(total, keepdims=True) / FEATURES + EPS)
+
+    def out(r):
+        piece = pl.ds(pl.multiple_of(r * lines, 8), lines)
+        return pltpu.make_async_copy(scaled.at[piece], hess_ref.at[piece], sems.at[r])
+
+    @pl.loop(0, row_count // lines)
+    def _(r):
+        row = lax.broadcasted_iota(jnp.int32, (lines, width), 0) + (tok * row_count - blk * width + r * lines)
+        column = lax.broadcasted_iota(jnp.int32, (lines, width), 1)
+        block = acc[pl.ds(pl.multiple_of(skew + r * lines, 8), lines), :] * inverse
+        scaled[pl.ds(pl.multiple_of(r * lines, 8), lines), :] = block + jnp.where(row == column, DAMP, 0.0)
+        out(r).start()
+
+    top_ref[...] = jnp.max(most, keepdims=True) * inverse
     for b in range(blocks):
 
         @pl.when(blk == b)
         def _():
+            whole = [None] * (width // LANES)
             for i in range(groups):
                 first = i * row_count
                 if first // width == b:
                     offset = first % width
-                    begin = min(offset // LANES * LANES, width - window)
-                    most = ratio_ref[:, begin : begin + window]
-                    for k in range(blocks):
-                        most = jnp.maximum(most, peaks[i * blocks + k])
-                    ratio_ref[:, begin : begin + window] = most
+                    begin = min(offset // LANES * LANES, width - window) // LANES
+                    for j in range(window // LANES):
+                        for k in range(blocks):
+                            value = notes[i * blocks + k, :, j * LANES : (j + 1) * LANES]
+                            old = whole[begin + j]
+                            whole[begin + j] = value if old is None else jnp.maximum(old, value)
+            ratio_ref[...] = (jnp.concatenate(whole, axis=1) * inverse).reshape(width)
+
+    @pl.loop(0, row_count // lines)
+    def _(r):
+        out(r).wait()
 
 
 def per_device(activations, signs):
@@ -468,48 +537,60 @@
     groups, blocks = lax.axis_size("tok"), lax.axis_size("blk")
     depth = 4 if groups % 8 == 0 else 1
     across = groups // (2 * depth)
-    sub, early, lag = 16, 1, 2
+    sub, early, lag = 16, 1, 3
     steps = tok_rows // sub
     row_count = FEATURES // groups
     window = window_size(groups, row_count, width)
     count, chips, tokens = groups * blocks, groups // 2, groups * tok_rows
+    lines = max(t for t in range(8, 65, 8) if row_count % t == 0)
     high, low = unit_tables()
     dma = pltpu.SemaphoreType.DMA
-    anywhere = pl.BlockSpec(memory_space=pl.ANY)
+    hbm = pl.BlockSpec(memory_space=pltpu.HBM)
     vmem = pl.BlockSpec(memory_space=pltpu.VMEM)
-    hessian, ratio, top = pl.pallas_call(
+    gram, notes = pl.pallas_call(
         functools.partial(kernel, depth, across, sub, early, lag, row_count),
         out_shape=(
-            jax.ShapeDtypeStruct((row_count, width), jnp.float32),
-            jax.ShapeDtypeStruct((1, width + window), jnp.float32),
-            jax.ShapeDtypeStruct((8, LANES), jnp.float32),
+            jax.ShapeDtypeStruct((window, width), jnp.float32),
+            jax.ShapeDtypeStruct((count + 1, 1, window + LANES), jnp.float32),
         ),
-        in_specs=[anywhere] * 4,
-        out_specs=(vmem, vmem, vmem),
+        in_specs=[hbm] * 4,
+        out_specs=(vmem, vmem),
         scratch_shapes=[
             pltpu.VMEM((tokens, width), jnp.bfloat16),
             pltpu.VMEM((tokens, window), jnp.bfloat16),
             pltpu.VMEM((blocks, tok_rows, width), jnp.bfloat16),
-            pltpu.VMEM((blocks + 1, 1, width), jnp.float32),
+        ]
+        + [pltpu.VMEM((width + 1024,), jnp.float32)] * blocks
+        + [
             pltpu.VMEM((UNIT, UNIT), jnp.bfloat16),
             pltpu.VMEM((UNIT, UNIT), jnp.bfloat16),
             pltpu.VMEM((blocks * (width // UNIT) * sub, UNIT), jnp.bfloat16),
-            pltpu.VMEM((window, width), jnp.float32),
             pltpu.VMEM((window, 2 * tok_rows), jnp.bfloat16),
             pltpu.VMEM((8, LANES), jnp.float32),
-            pltpu.VMEM((count, 8, LANES), jnp.float32),
             pltpu.VMEM((window, LANES), jnp.float32),
-            pltpu.VMEM((count + 1, 1, window), jnp.float32),
             dma((2,)), dma, dma, dma, dma((blocks,)), dma, dma((blocks * steps,)),
             dma((chips * steps,)), dma, dma((chips,)), dma((2,)), dma((2,)), dma((2 * blocks,)), dma((chips,)),
-            dma, dma, dma, dma,
+            dma, dma,
         ],
         compiler_params=pltpu.CompilerParams(
-            collective_id=0, has_side_effects=True, vmem_limit_bytes=56 * 1024 * 1024
+            collective_id=0, has_side_effects=True, vmem_limit_bytes=36 * 1024 * 1024
         ),
         name="fused",
-    )(activations, signs.reshape(1, width), jnp.asarray(high), jnp.asarray(low))
-    return hessian, ratio[0, :width], top[0, 0]
+    )(activations, signs, jnp.asarray(high), jnp.asarray(low))
+    hessian, ratio, top = pl.pallas_call(
+        functools.partial(finish_kernel, row_count, lines),
+        out_shape=(
+            jax.ShapeDtypeStruct((row_count, width), jnp.float32),
+            jax.ShapeDtypeStruct((width,), jnp.float32),
+            jax.ShapeDtypeStruct((1, 1), jnp.float32),
+        ),
+        in_specs=[vmem, vmem],
+        out_specs=(hbm, vmem, vmem),
+        scratch_shapes=[pltpu.VMEM((row_count, width), jnp.float32), dma((row_count // lines,))],
+        compiler_params=pltpu.CompilerParams(vmem_limit_bytes=24 * 1024 * 1024),
+        name="finish",
+    )(gram, notes)
+    return hessian, ratio, top.reshape(())
 
 
 def solution(mesh):

time: 118 us -> 106 us (0.90)
  Pallas kernels: 107 us -> 100 us
  local copies, waits for them, and re-layouts: 9.87 us -> 4.73 us
    pallas_call x1, Pallas kernels: 107 us -> 96.6 us  [per_device(): pl.pallas_call(functools.partial(kernel, depth, across, sub, early, lag,...]
    pallas_call x0 -> x1, Pallas kernels: none -> 3.65 us  [per_device(): pl.pallas_call(functools.partial(finish_kernel, row_count, lines), out_sh...]
    slice x2 -> x0, local copies, waits for them, and re-layouts: 2.54 us -> none  [per_device(): return (hessian, ratio[0, :width], top[0, 0])]
    reshape x1 -> x0, local copies, waits for them, and re-layouts: 1.33 us -> none  [per_device(): signs.reshape(1, width)]
    unnamed x1 -> x8, local copies, waits for them, and re-layouts: 5.99 us -> 4.73 us
where the time goes in v2:
time: 106 us
  Pallas kernels  100 us (94%)
  local copies, waits for them, and re-layouts  4.73 us (4%)
    pallas_call x1, Pallas kernels, per_device(): pl.pallas_call(functools.partial(kernel, depth, across, sub, early, lag,...  96.6 us
    unnamed x8, local copies, waits for them, and re-layouts  4.73 us
    pallas_call x1, Pallas kernels, per_device(): pl.pallas_call(functools.partial(finish_kernel, row_count, lines), out_sh...  3.65 us

profile of v2, /device:TPU:0, one launch (start us, length us, event | category | flops | bytes accessed | tf_op | source)
XLA Modules:
  0.0 105.6 jit_solution(10570742337292374804)
XLA Ops:
  0.6 0.0 copy-start
  0.6 1.4 %copy-done = bf16[896,896]{1,0:T(8,128)(2,1)S(1)} copy-done((bf16[896,896]{1,0:T(8,128)(2,1)S(1)}, bf16[896,896]{1,0:T(8,128)(2,1)}, u32[]{:S(2)}) %copy-start) | copy-done | bytes 1605656
  2.1 0.0 copy-start.1
  2.1 1.4 %copy-done.1 = bf16[896,896]{1,0:T(8,128)(2,1)S(1)} copy-done((bf16[896,896]{1,0:T(8,128)(2,1)S(1)}, bf16[896,896]{1,0:T(8,128)(2,1)}, u32[]{:S(2)}) %copy-start.1) | copy-done | bytes 1605656
  3.5 0.0 copy-start.2
  3.5 1.2 %copy-done.2 = bf16[128,3584]{1,0:T(8,128)(2,1)S(1)} copy-done((bf16[128,3584]{1,0:T(8,128)(2,1)S(1)}, bf16[128,3584]{1,0:T(8,128)(2,1)}, u32[]{:S(2)}) %copy-start.2) | copy-done | bytes 917528
  4.7 0.0 copy-start.3
  4.7 0.7 copy-done.3
  5.4 96.6 %fused.1 = (f32[512,3584]{1,0:T(8,128)S(1)}, f32[33,1,640]{2,1,0:T(1,128)S(1)}) custom-call(bf16[128,3584]{1,0:T(8,128)(2,1)S(1)} %copy-done.2, f32[3584]{0:T(1024)S(1)} %copy-done.3, bf16[896,896]{1,0:T(8,128)(2,1)S(1)} %copy-done.1, bf16[896,896]{1,0:T(8,128)(2,1)S(1)} %copy-done), custom_call_target="tpu_custom_call" | custom-call | tf_op jit(solution)/shard_map/fused/pallas_call | solution.py:550
  102.0 3.7 %finish.1 = (f32[448,3584]{1,0:T(8,128)}, f32[3584]{0:T(1024)}, f32[1,1]{1,0:T(1,128)}) custom-call(f32[512,3584]{1,0:T(8,128)S(1)} %get-tuple-element.8.acc, f32[33,1,640]{2,1,0:T(1,128)S(1)} %get-tuple-element.9.notes), custom_call_target="tpu_custom_call" | custom-call | tf_op jit(solution)/shard_map/finish/pallas_call | solution.py:580
Async XLA Ops:
  0.6 1.4 %copy-start = (bf16[896,896]{1,0:T(8,128)(2,1)S(1)}, bf16[896,896]{1,0:T(8,128)(2,1)}, u32[]{:S(2)}) copy-start(bf16[896,896]{1,0:T(8,128)(2,1)} %constant.5.clone.low_hbm) | copy-start | bytes 4816900
  2.1 1.4 %copy-start.1 = (bf16[896,896]{1,0:T(8,128)(2,1)S(1)}, bf16[896,896]{1,0:T(8,128)(2,1)}, u32[]{:S(2)}) copy-start(bf16[896,896]{1,0:T(8,128)(2,1)} %constant.4.clone.high_hbm) | copy-start | bytes 4816900
  3.5 1.2 %copy-start.2 = (bf16[128,3584]{1,0:T(8,128)(2,1)S(1)}, bf16[128,3584]{1,0:T(8,128)(2,1)}, u32[]{:S(2)}) copy-start(bf16[128,3584]{1,0:T(8,128)(2,1)} %x_ref.1) | copy-start | bytes 2752516
  4.7 0.7 copy-start.3
